TPU v7x, 512 devices: a 8x2x16 block of a 8x8x16 slice. The times are simulated.
512 devices in a mesh: replica: 2 (over y), kv: 16 (over z), head: 8 (over x), sub: 2 (over core).
Axes of the slice: x: 8, y: 2, z: 16, core: 2. Of those that a mesh axis runs over, the one named last changes fastest.
The devices are a block of a 8x8x16 slice.
Arguments:
- queries: bfloat16 [1024, 64, 128], P(('replica', 'kv'), 'head'), parts along dimension 0, may hold values from -12 to 12
- sys_keys: bfloat16 [16, 4096, 128], P(('replica', 'head'), ('kv', 'sub')), parts along dimension 0, may hold values from -5 to 5
- sys_values: bfloat16 [16, 4096, 128], P(('replica', 'head'), ('kv', 'sub')), parts along dimension 0, may hold values from -6 to 6
- task_keys: bfloat16 [32, 8, 4096, 128], P(('replica', 'kv'), 'head', 'sub'), parts along dimension 0, may hold values from -5 to 5
- task_values: bfloat16 [32, 8, 4096, 128], P(('replica', 'kv'), 'head', 'sub'), parts along dimension 0, may hold values from -6 to 6
- suffix_keys: bfloat16 [1024, 8, 512, 128], P(('replica', 'kv', 'sub'), 'head'), parts along dimension 0, may hold values from -5 to 5
- suffix_values: bfloat16 [1024, 8, 512, 128], P(('replica', 'kv', 'sub'), 'head'), parts along dimension 0, may hold values from -6 to 6
- task_ids: int32 [1024], P(('replica', 'kv')), parts along dimension 0, may hold values from 0 to 15, as said below
- suffix_len: int32 [1024], P(('replica', 'kv', 'sub')), parts along dimension 0, may hold values from 256 to 512, as said below
Outputs:
- attended: bfloat16 [1024, 64, 128], P(('replica', 'kv', 'sub'), 'head'), parts along dimension 0
There are 2 independent parts, one for each index of `replica`. A program takes and returns all parts, laid end to end along the dimension named above; each array names one. Nothing has to cross between parts.
Inputs may be any that keep to these rules, and one draw needn't show every extreme that they name: `task_ids`: task t's prefix is task_keys[t]. The rows 2 * 16 * p to 2 * 16 * (p + 1) - 1 form aligned blocks; in each block no task is named more than 8 times, and one task, the same for all blocks, is named exactly 8 times in every block. `suffix_len`: each aligned block of 16 rows holds one length equal to 512.
All inputs are finite; a program needn't handle non-finite values.
Results may differ from a plain program's by a relative error of at most 0.005.
Values may be sent and summed in bfloat16 or wider, within the bound.
A program may use at most 64 MiB of HBM per device.

v0:
```python
import math

import jax
import jax.numpy as jnp
from jax import lax
from jax.sharding import PartitionSpec as P

CAP = 8


NEGATIVE = -1e30


def sent_together(arrays, axis, dim, along):
    widths = [a.shape[along] for a in arrays]
    both = jnp.concatenate(arrays, axis=along)
    out = lax.all_gather(both, axis, axis=dim, tiled=True)
    return tuple(jnp.split(out, [sum(widths[:k]) for k in range(1, len(widths))], axis=along))


def in_one_piece(arrays, axis, split_dim, concat_dim, along):
    columns = [a.reshape(*a.shape[:along], -1) for a in arrays]
    both = jnp.concatenate(columns, axis=along)
    out, at, outs = (
        lax.all_to_all(both, axis, split_axis=split_dim, concat_axis=concat_dim, tiled=True),
        0,
        [],
    )
    for a, column in zip(arrays, columns):
        section = out[..., at : at + column.shape[along]]
        outs.append(section.reshape(*section.shape[:along], *a.shape[along:]))
        at += column.shape[along]
    return tuple(outs)


def shared_partial(query_rows, level_keys, level_values):
    score_scale = 1.0 / math.sqrt(query_rows.shape[-1])
    scores = (
        jnp.einsum("rkgd,kld->rkgl", query_rows, level_keys, preferred_element_type=jnp.float32)
        * score_scale
    )
    maxima = jnp.max(scores, axis=3)
    weights = jnp.exp(scores - maxima[..., None])
    totals = jnp.sum(weights, axis=3)
    numerator = jnp.einsum(
        "rkgl,kld->rkgd",
        weights.astype(jnp.bfloat16),
        level_values,
        preferred_element_type=jnp.float32,
    )
    return (maxima, totals, numerator)


def suffix_partial(query_rows, own_keys, own_values, lengths):
    score_scale = 1.0 / math.sqrt(query_rows.shape[-1])
    scores = (
        jnp.einsum("rkgd,rkld->rkgl", query_rows, own_keys, preferred_element_type=jnp.float32)
        * score_scale
    )
    positions = lax.broadcasted_iota(jnp.int32, scores.shape, 3)
    usable = positions < lengths[:, None, None, None]
    scores = jnp.where(usable, scores, NEGATIVE)
    maxima = jnp.max(scores, axis=3)
    weights = jnp.where(usable, jnp.exp(scores - maxima[..., None]), 0.0)
    totals = jnp.sum(weights, axis=3)
    numerator = jnp.einsum(
        "rkgl,rkld->rkgd",
        weights.astype(jnp.bfloat16),
        own_values,
        preferred_element_type=jnp.float32,
    )
    return (maxima, totals, numerator)


def combine(earlier_part, later_part):
    maxima = jnp.maximum(earlier_part[0], later_part[0])
    earlier_factor = jnp.exp(earlier_part[0] - maxima)
    later_factor = jnp.exp(later_part[0] - maxima)
    return (
        maxima,
        earlier_part[1] * earlier_factor + later_part[1] * later_factor,
        earlier_part[2] * earlier_factor[..., None] + later_part[2] * later_factor[..., None],
    )


def fold_sources(partials):
    maxima = jnp.max(partials[0], axis=0)
    factor = jnp.exp(partials[0] - maxima)
    return (
        maxima,
        jnp.sum(partials[1] * factor, axis=0),
        jnp.sum(partials[2] * factor[..., None], axis=0),
    )


def split_lead(partials, blocks):
    return tuple(
        (
            member.reshape((blocks, member.shape[0] // blocks) + member.shape[1:])
            for member in partials
        )
    )


def body(
    queries,
    sys_keys,
    sys_values,
    task_keys,
    task_values,
    suffix_keys,
    suffix_values,
    task_ids,
    suffix_len,
):
    pair_rows, head_count, head_dim = queries.shape
    kv_heads = sys_keys.shape[0]
    group_size = head_count // kv_heads
    own_rows = suffix_keys.shape[0]
    owners = lax.axis_size("kv")
    halves_count = lax.axis_size("sub")
    pair_query = queries.reshape(pair_rows, kv_heads, group_size, head_dim)
    own_query = lax.dynamic_slice_in_dim(pair_query, lax.axis_index("sub") * own_rows, own_rows, 0)
    start_state = (
        jnp.full((pair_rows, kv_heads, group_size), NEGATIVE, jnp.float32),
        jnp.zeros((pair_rows, kv_heads, group_size), jnp.float32),
        jnp.zeros((pair_rows, kv_heads, group_size, head_dim), jnp.float32),
    )
    pieces = sent_together((sys_keys, sys_values), "kv", 1, 0)
    system_part = combine(start_state, shared_partial(pair_query, pieces[0], pieces[1]))
    row_index = lax.broadcasted_iota(jnp.int32, (pair_rows, pair_rows), 0)
    column_index = lax.broadcasted_iota(jnp.int32, (pair_rows, pair_rows), 1)
    same_before = (task_ids[:, None] == task_ids[None, :]) & (column_index < row_index)
    places = task_ids * CAP + jnp.sum(same_before.astype(jnp.int32), axis=1)
    outgoing = (
        jnp.zeros((owners * CAP, kv_heads, group_size, head_dim), jnp.bfloat16)
        .at[places]
        .set(pair_query)
    )
    outgoing = outgoing.reshape(owners, CAP, kv_heads, group_size, head_dim)
    own_task_keys = task_keys[0]
    own_task_values = task_values[0]
    arrived = lax.all_to_all(outgoing, "kv", split_axis=0, concat_axis=0, tiled=True)
    sources = arrived.shape[0]
    slot_count = arrived.shape[1]
    stacked = arrived.reshape((sources * slot_count,) + arrived.shape[2:])
    parted_task = split_lead(shared_partial(stacked, own_task_keys, own_task_values), sources)
    returned = (
        lax.all_to_all(parted_task[0], "kv", split_axis=0, concat_axis=0, tiled=True),
        lax.all_to_all(parted_task[1], "kv", split_axis=0, concat_axis=0, tiled=True),
        lax.all_to_all(parted_task[2], "kv", split_axis=0, concat_axis=0, tiled=True),
    )
    task_part = tuple(
        (
            jnp.take(member.reshape((owners * CAP,) + member.shape[2:]), places, axis=0)
            for member in returned
        )
    )
    pair_part = combine(system_part, task_part)
    split_pair = split_lead(pair_part, halves_count)
    both_halves = fold_sources(
        in_one_piece((split_pair[0], split_pair[1], split_pair[2]), "sub", 0, 0, 4)
    )
    whole = combine(both_halves, suffix_partial(own_query, suffix_keys, suffix_values, suffix_len))
    attended = whole[2] / whole[1][..., None]
    return attended.reshape(own_rows, head_count, head_dim).astype(jnp.bfloat16)


def solution(mesh):
    in_specs = (
        P(("replica", "kv"), "head", None),
        P(("replica", "head"), ("kv", "sub"), None),
        P(("replica", "head"), ("kv", "sub"), None),
        P(("replica", "kv"), "head", "sub", None),
        P(("replica", "kv"), "head", "sub", None),
        P(("replica", "kv", "sub"), "head", None, None),
        P(("replica", "kv", "sub"), "head", None, None),
        P(("replica", "kv")),
        P(("replica", "kv", "sub")),
    )
    out_specs = P(("replica", "kv", "sub"), "head", None)
    return jax.shard_map(body, mesh=mesh, in_specs=in_specs, out_specs=out_specs, check_vma=False)
```

profile of v0, /device:TPU:65, one launch (start us, length us, event | category | flops | bytes accessed | tf_op | source)
XLA Modules:
  0.0 170.5 jit_solution(2766319380264371584)
XLA Ops:
  6.6 1.0 convert_reduce_fusion
  7.5 0.7 compare_and_fusion
  8.3 2.5 %scatter_fusion = bf16[128,8,128]{2,1,0:T(8,128)(2,1)S(1)} fusion(bf16[128,8,128]{2,1,0:T(8,128)(2,1)S(1)} %broadcast.157, s32[32]{0:T(128)S(1)} %get-tuple-element.10, bf16[32,8,128]{2,1,0:T(8,128)(2,1)} %param.11), kind=kCustom, calls=%fused_computation.3 | custom fusion | bytes 196736 | tf_op jit(solution)/shard_map/scatter | solution.py:138
  10.8 0.7 copy.116
  11.6 44.2 %all-to-all-start = ((bf16[16,8,1,8,128]{4,1,3,2,0:T(8,128)(2,1)}), bf16[16,8,1,8,128]{4,1,3,2,0:T(8,128)(2,1)S(1)}, u32[]{:S(2)}, u32[]{:S(2)}) async-start(bf16[16,8,1,8,128]{4,1,3,2,0:T(8,128)(2,1)} %copy.116), calls=%async_computation | async-start | bytes 524288 | tf_op jit(solution)/shard_map/all_to_all | solution.py:143
  55.9 1.4 pad_maximum_fusion.1
  57.3 12.0 %all-to-all-done = bf16[16,8,1,8,128]{4,1,3,2,0:T(8,128)(2,1)S(1)} async-done(((bf16[16,8,1,8,128]{4,1,3,2,0:T(8,128)(2,1)}), bf16[16,8,1,8,128]{4,1,3,2,0:T(8,128)(2,1)S(1)}, u32[]{:S(2)}, u32[]{:S(2)}) %all-to-all-start) | async-done | bytes 262176 | tf_op jit(solution)/shard_map/all_to_all | solution.py:143
  69.4 2.4 %bitcast_reduce_fusion = (f32[128,8]{0,1:T(8,128)S(1)}, f32[128,8,2048]{2,0,1:T(8,128)S(1)}) fusion(bf16[1,1,2048,128]{3,2,1,0:T(8,128)(2,1)} %param.14, bf16[16,8,1,8,128]{4,1,3,2,0:T(8,128)(2,1)S(1)} %all-to-all-done), kind=kOutput, calls=%fused_computation.5 | convolution fusion | flops 541064192 | bytes 9179136 | tf_op jit(solution)/shard_map/rkgd,kld->rkgl/dot_general | solution.py:39
  71.7 3.2 %copy-done.1 = f32[128,8,2048]{2,0,1:T(8,128)} copy-done((f32[128,8,2048]{2,0,1:T(8,128)}, f32[128,8,2048]{2,0,1:T(8,128)S(1)}, u32[]{:S(2)}) %copy-start.1) | copy-done | bytes 8388632
  74.9 1.6 fusion.2
  76.6 0.7 copy.141
  77.3 10.5 %all-to-all-start.2 = ((f32[16,8,1,8]{3,1,2,0:T(8,128)}), f32[16,8,1,8]{3,1,2,0:T(8,128)S(1)}, u32[]{:S(2)}, u32[]{:S(2)}) async-start(f32[16,8,1,8]{3,1,2,0:T(8,128)} %bitcast.20), calls=%async_computation.2 | async-start | bytes 131072 | tf_op jit(solution)/shard_map/all_to_all | solution.py:150
  88.6 10.8 %all-to-all-done.2 = f32[16,8,1,8]{3,1,2,0:T(8,128)S(1)} async-done(((f32[16,8,1,8]{3,1,2,0:T(8,128)}), f32[16,8,1,8]{3,1,2,0:T(8,128)S(1)}, u32[]{:S(2)}, u32[]{:S(2)}) %all-to-all-start.2) | async-done | bytes 4128 | tf_op jit(solution)/shard_map/all_to_all | solution.py:150
  99.4 4.6 %all-to-all-start.1 = ((f32[16,8,1,8]{1,3,2,0:T(8,128)}), f32[16,8,1,8]{1,3,2,0:T(8,128)S(1)}, u32[]{:S(2)}, u32[]{:S(2)}) async-start(f32[16,8,1,8]{1,3,2,0:T(8,128)} %copy.118), calls=%async_computation.1 | async-start | bytes 131072 | tf_op jit(solution)/shard_map/all_to_all | solution.py:149
  104.0 4.8 %fusion.13 = f32[16,8,1,8,128]{4,1,0,3,2:T(8,128)S(1)} fusion(f32[128,8,2048]{2,0,1:T(8,128)} %copy-done.1, f32[128,8]{0,1:T(8,128)S(1)} %get-tuple-element.22, bf16[1,1,2048,128]{3,2,1,0:T(8,128)(2,1)S(1)} %copy-done.3), kind=kOutput, calls=%fused_computation.20 | convolution fusion | flops 543162368 | bytes 9441280 | tf_op jit(solution)/shard_map/rkgl,kld->rkgd/dot_general | solution.py:45
  108.9 0.9 copy.123
  109.7 6.2 %all-to-all-done.1 = f32[16,8,1,8]{1,3,2,0:T(8,128)S(1)} async-done(((f32[16,8,1,8]{1,3,2,0:T(8,128)}), f32[16,8,1,8]{1,3,2,0:T(8,128)S(1)}, u32[]{:S(2)}, u32[]{:S(2)}) %all-to-all-start.1) | async-done | bytes 4128 | tf_op jit(solution)/shard_map/all_to_all | solution.py:149
  115.9 5.3 %all-to-all-start.3 = ((f32[16,8,1,8,128]{4,1,3,2,0:T(8,128)}), f32[16,8,1,8,128]{4,1,3,2,0:T(8,128)S(1)}, u32[]{:S(2)}, u32[]{:S(2)}) async-start(f32[16,8,1,8,128]{4,1,3,2,0:T(8,128)} %copy.123), calls=%async_computation.3 | async-start | bytes 1048576 | tf_op jit(solution)/shard_map/all_to_all | solution.py:151
  121.2 0.7 fusion.84
  122.0 0.7 copy.133
  122.9 0.7 copy.139
  124.7 0.7 all-gather.2.cloned.1.call-done
  125.5 2.8 %fusion.83 = (f32[32,8]{0,1:T(8,128)S(1)}, f32[32,1,8,2048]{3,0,2,1:T(8,128)}) fusion(bf16[32,8,128]{2,1,0:T(8,128)(2,1)S(1)} %copy-done.2, bf16[2,2048,128]{2,1,0:T(8,128)(2,1)} %all-gather.2.cloned.1.call-done), kind=kOutput, calls=%fused_computation.101 | convolution fusion | flops 135266048 | bytes 2688000 | tf_op jit(solution)/shard_map/rkgd,kld->rkgl/dot_general | solution.py:39
  128.4 2.0 %fusion.12 = f32[32,8]{0,1:T(8,128)S(1)} fusion(f32[32,1,8,2048]{3,0,2,1:T(8,128)} %get-tuple-element.21, f32[32,8]{0,1:T(8,128)S(1)} %get-tuple-element.20), kind=kLoop, calls=%fused_computation.19 | loop fusion | flops 1048320 | bytes 2099200 | tf_op jit(solution)/shard_map/reduce_sum | solution.py:44
  130.6 0.7 copy.126
  131.6 0.9 copy.128
  133.1 12.5 %all-to-all-done.3 = f32[16,8,1,8,128]{4,1,3,2,0:T(8,128)S(1)} async-done(((f32[16,8,1,8,128]{4,1,3,2,0:T(8,128)}), f32[16,8,1,8,128]{4,1,3,2,0:T(8,128)S(1)}, u32[]{:S(2)}, u32[]{:S(2)}) %all-to-all-start.3) | async-done | bytes 524320 | tf_op jit(solution)/shard_map/all_to_all | solution.py:151
  145.7 0.7 gather_fusion
  146.4 2.2 %fusion.26 = f32[32,1,8,128]{3,0,2,1:T(8,128)S(1)} fusion(f32[32,1,8,2048]{3,0,2,1:T(8,128)} %get-tuple-element.21, f32[32,8]{0,1:T(8,128)S(1)} %get-tuple-element.20, bf16[2,2048,128]{2,1,0:T(8,128)(2,1)} %all-gather.2.cloned.1.call-done, f32[32,8,128]{2,1,0:T(8,128)S(1)} %gather_fusion, f32[32,8]{0,1:T(8,128)} %copy.126, f32[32,8]{0,1:T(8,128)S(1)} %copy.122, ...), kind=kOutput, calls=%fused_computation.28 | convolution fusion | flops 135462912 | bytes 2898432 | tf_op jit(solution)/shard_map/rkgl,kld->rkgd/dot_general | solution.py:45
  148.7 1.1 pad_maximum_fusion
  149.8 10.1 %all_to_all.25 = f32[2,16,1,8,130]{4,3,2,1,0:T(8,128)S(1)} all-to-all(f32[2,16,1,8,130]{4,3,2,1,0:T(8,128)S(1)} %pad_maximum_fusion), channel_id=1, replica_groups=mesh['replica'=2,'kv'=16,'head'=8,'sub'=2] {'sub'}, dimensions={0} | all-to-all | bytes 266240 | tf_op jit(solution)/shard_map/all_to_all | solution.py:25
  161.0 2.7 %fusion.36 = bf16[16,8,128]{2,1,0:T(8,128)(2,1)} fusion(bf16[16,1,512,128]{3,2,1,0:T(8,128)(2,1)} %param.17, f32[16,8,512]{2,1,0:T(8,128)S(1)} %get-tuple-element.25, f32[16,8]{1,0:T(8,128)S(1)} %get-tuple-element.24, s32[16]{0:T(128)S(1)} %copy-done.9, f32[16,8,128]{2,1,0:T(8,128)S(1)} %fusion.50, f32[16,8]{1,0:T(8,128)S(1)} %copy.140, ...), kind=kOutput, calls=%fused_computation.32 | convolution fusion | flops 17121280 | bytes 2459712 | tf_op jit(solution)/shard_map/rkgl,rkld->rkgd/dot_general | solution.py:66
  (49 shorter events, 4.7 us)
Async XLA Ops:
  6.5 114.7 %copy-start = (bf16[16,1,512,128]{3,2,1,0:T(8,128)(2,1)S(1)}, bf16[16,1,512,128]{3,2,1,0:T(8,128)(2,1)}, u32[]{:S(2)}) copy-start(bf16[16,1,512,128]{3,2,1,0:T(8,128)(2,1)} %param.16) | copy-start | bytes 6291460
  8.2 122.3 %copy-start.7 = (pred[32]{0:T(512)(128)(4,1)}, pred[32]{0:T(512)(128)(4,1)S(1)}, u32[]{:S(2)}) copy-start(pred[32]{0:T(512)(128)(4,1)S(1)} %get-tuple-element.9) | copy-start | bytes 100
  11.6 57.8 %all-to-all-start = ((bf16[16,8,1,8,128]{4,1,3,2,0:T(8,128)(2,1)}), bf16[16,8,1,8,128]{4,1,3,2,0:T(8,128)(2,1)S(1)}, u32[]{:S(2)}, u32[]{:S(2)}) async-start(bf16[16,8,1,8,128]{4,1,3,2,0:T(8,128)(2,1)} %copy.116), calls=%async_computation | async-start | bytes 524288 | tf_op jit(solution)/shard_map/all_to_all | solution.py:143
  55.8 69.7 %all-gather.2.cloned.1.call-start = ((), (), s32[]{:S(2)}) async-start(), calls=%async_computation.5 | async-start | bytes 1114112 | tf_op jit(solution)/shard_map/all_gather | solution.py:17
  71.7 3.2 %copy-start.1 = (f32[128,8,2048]{2,0,1:T(8,128)}, f32[128,8,2048]{2,0,1:T(8,128)S(1)}, u32[]{:S(2)}) copy-start(f32[128,8,2048]{2,0,1:T(8,128)S(1)} %get-tuple-element.23) | copy-start | bytes 25165828
  74.9 29.1 %copy-start.3 = (bf16[1,1,2048,128]{3,2,1,0:T(8,128)(2,1)S(1)}, bf16[1,1,2048,128]{3,2,1,0:T(8,128)(2,1)}, u32[]{:S(2)}) copy-start(bf16[1,1,2048,128]{3,2,1,0:T(8,128)(2,1)} %param.15) | copy-start | bytes 1572868
  77.3 22.1 %all-to-all-start.2 = ((f32[16,8,1,8]{3,1,2,0:T(8,128)}), f32[16,8,1,8]{3,1,2,0:T(8,128)S(1)}, u32[]{:S(2)}, u32[]{:S(2)}) async-start(f32[16,8,1,8]{3,1,2,0:T(8,128)} %bitcast.20), calls=%async_computation.2 | async-start | bytes 131072 | tf_op jit(solution)/shard_map/all_to_all | solution.py:150
  99.4 16.6 %all-to-all-start.1 = ((f32[16,8,1,8]{1,3,2,0:T(8,128)}), f32[16,8,1,8]{1,3,2,0:T(8,128)S(1)}, u32[]{:S(2)}, u32[]{:S(2)}) async-start(f32[16,8,1,8]{1,3,2,0:T(8,128)} %copy.118), calls=%async_computation.1 | async-start | bytes 131072 | tf_op jit(solution)/shard_map/all_to_all | solution.py:149
  108.9 12.4 %copy-start.2 = (bf16[32,8,128]{2,1,0:T(8,128)(2,1)S(1)}, bf16[32,8,128]{2,1,0:T(8,128)(2,1)}, u32[]{:S(2)}) copy-start(bf16[32,8,128]{2,1,0:T(8,128)(2,1)} %param.11) | copy-start | bytes 196612
  108.9 12.4 %copy-start.8 = (s32[16]{0:T(128)S(1)}, s32[16]{0:T(128)}, u32[]{:S(2)}) copy-start(s32[16]{0:T(128)} %param.19) | copy-start | bytes 196
  115.9 29.6 %all-to-all-start.3 = ((f32[16,8,1,8,128]{4,1,3,2,0:T(8,128)}), f32[16,8,1,8,128]{4,1,3,2,0:T(8,128)S(1)}, u32[]{:S(2)}, u32[]{:S(2)}) async-start(f32[16,8,1,8,128]{4,1,3,2,0:T(8,128)} %copy.123), calls=%async_computation.3 | async-start | bytes 1048576 | tf_op jit(solution)/shard_map/all_to_all | solution.py:151
  123.5 6.9 %copy-start.6 = (s32[1024]{0:T(1024)}, s32[1024]{0:T(1024)S(1)}, u32[]{:S(2)}) copy-start(s32[1024]{0:T(1024)S(1)} %pad_clamp_fusion) | copy-start | bytes 12292
  146.4 14.1 %copy-start.4 = (f32[16,8]{0,1:T(8,128)S(1)}, f32[16,8]{0,1:T(8,128)}, u32[]{:S(2)}) copy-start(f32[16,8]{0,1:T(8,128)} %copy.133) | copy-start | bytes 1540
  146.4 14.1 %copy-start.5 = (f32[16,8]{0,1:T(8,128)S(1)}, f32[16,8]{0,1:T(8,128)}, u32[]{:S(2)}) copy-start(f32[16,8]{0,1:T(8,128)} %copy.139) | copy-start | bytes 1540
  146.4 14.5 %copy-start.9 = (s32[16]{0:T(128)S(1)}, s32[16]{0:T(128)}, u32[]{:S(2)}) copy-start(s32[16]{0:T(128)} %param.19) | copy-start | bytes 196
Sparse Core Ops, SparseCore 0:
  58.7 66.7 all-gather.1
where the time goes:
time: 171 us; the launch traced here: 170 us
  starting transfers between devices  64.7 us (38%)
  waiting for transfers between devices  42.4 us (25%)
  matrix products  15.6 us (9%)
  local copies, waits for them, and re-layouts  15.1 us (9%)
  between operations  13.7 us (8%)
  blocking collectives  10.1 us (6%)
  other arithmetic  9.03 us (5%)
    all_to_all x1, starting transfers between devices, body(): lax.all_to_all(outgoing, 'kv', split_axis=0, concat_axis=0, tiled=True)  44.2 us
    all_to_all x1, waiting for transfers between devices, body(): lax.all_to_all(parted_task[2], 'kv', split_axis=0, concat_axis=0, tiled=T...  12.5 us
    all_to_all x1, waiting for transfers between devices, body(): lax.all_to_all(outgoing, 'kv', split_axis=0, concat_axis=0, tiled=True)  12 us
    all_to_all x1, waiting for transfers between devices, body(): lax.all_to_all(parted_task[1], 'kv', split_axis=0, concat_axis=0, tiled=T...  10.8 us
    all_to_all x1, starting transfers between devices, body(): lax.all_to_all(parted_task[1], 'kv', split_axis=0, concat_axis=0, tiled=T...  10.5 us
    all_to_all x1, blocking collectives, in_one_piece(): lax.all_to_all(both, axis, split_axis=split_dim, concat_axis=concat_dim,...  10.1 us
    dot_general x2, matrix products, shared_partial(): jnp.einsum('rkgl,kld->rkgd', weights.astype(jnp.bfloat16), level_values,...  7.03 us
    all_to_all x1, waiting for transfers between devices, body(): lax.all_to_all(parted_task[0], 'kv', split_axis=0, concat_axis=0, tiled=T...  6.21 us
  transfers between devices with their start and end apart: 5, of which 5 were waited for; matrix products, arithmetic and copies ran while one was open for 14% of the time, Pallas kernels for 0%

commit v1 on v0

v1 whole, which is shorter than its diff:
```python
import functools
import math

import jax
import jax.numpy as jnp
from jax import lax
from jax.experimental import pallas as pl
from jax.experimental.pallas import tpu as pltpu
from jax.sharding import PartitionSpec as P

CAP = 8
NEGATIVE = -1e30
MESH = pl.DeviceIdType.MESH
F32 = jnp.float32
BF16 = jnp.bfloat16


def nt_dot(a, b):
    return lax.dot_general(a, b, (((1,), (1,)), ((), ())), preferred_element_type=F32)


def nn_dot(a, b):
    return lax.dot_general(a, b, (((1,), (0,)), ((), ())), preferred_element_type=F32)


def iota(shape, dim):
    return lax.broadcasted_iota(jnp.int32, shape, dim)


def kernel(
    n,
    heads,
    q_hbm,
    sk_hbm,
    sv_hbm,
    tk_hbm,
    tv_hbm,
    uk_hbm,
    uv_hbm,
    ids_ref,
    len_ref,
    out_ref,
    qv,
    kall,
    vall,
    tk,
    tv,
    uk,
    uv,
    qs,
    qr,
    rs,
    rr,
    ss,
    sr,
    gmat,
    scores,
    sys_m,
    sys_l,
    sys_acc,
    suf_l,
    suf_o,
    xs,
    xr,
    local_sem,
    ring_send,
    ring_recv,
    q_send,
    q_recv,
    r_send,
    r_recv,
    s_send,
    s_recv,
    t_send,
    t_recv,
    x_send,
    x_recv,
):
    z = lax.axis_index("kv")
    c = lax.axis_index("sub")
    half = n // 2
    rows, hd = q_hbm.shape
    pair = rows // heads
    own = rows // 2
    own_seqs = uk_hbm.shape[0]
    suf = uk_hbm.shape[1]
    task_half = tk_hbm.shape[0]
    slots = CAP // 2
    hb = slots * heads
    per = hd // hb
    unit = math.log2(math.e) / math.sqrt(hd)

    order = [0]
    for d in range(1, half):
        order += [d, n - d]
    order.append(half)
    place = {o: k for k, o in enumerate(order)}

    def at(offset):
        return place[offset % n]

    def kv_dev(offset):
        return {"kv": lax.rem(z + (offset % n), n)}

    partner = {"sub": 1 - c}

    loads = []
    for i, (src, dst) in enumerate(
        (
            (q_hbm, qv),
            (sk_hbm, kall.at[0]),
            (sv_hbm, vall.at[0]),
            (uk_hbm, uk),
            (uv_hbm, uv),
            (tk_hbm, tk.at[0]),
            (tv_hbm, tv.at[0]),
        )
    ):
        copy = pltpu.make_async_copy(src, dst, local_sem.at[i])
        copy.start()
        loads.append(copy)

    barrier = pltpu.get_barrier_semaphore()
    pl.semaphore_signal(barrier, inc=1, device_id=partner, device_id_type=MESH)
    for o in order[1:]:
        pl.semaphore_signal(barrier, inc=1, device_id=kv_dev(o), device_id_type=MESH)

    ids_row = ids_ref[...].astype(F32)
    ids_b = jnp.broadcast_to(ids_row, (pair, pair))
    eye = iota((pair, pair), 0) == iota((pair, pair), 1)
    ids_col = jnp.sum(jnp.where(eye, ids_b, 0.0), axis=1, keepdims=True)
    before = iota((pair, pair), 0) < iota((pair, pair), 1)
    same = jnp.logical_and(ids_col == ids_b, before)
    rank_row = jnp.sum(jnp.where(same, 1.0, 0.0), axis=0, keepdims=True)
    code_row = ids_row * CAP + rank_row
    code_b = jnp.broadcast_to(code_row, (pair, pair))
    spread = (iota((rows, pair), 0) // heads == iota((rows, pair), 1))
    code_col = jnp.sum(
        jnp.where(spread, jnp.broadcast_to(code_row, (rows, pair)), 0.0), axis=1, keepdims=True
    )
    spread_t = jnp.where(iota((pair, rows), 1) // heads == iota((pair, rows), 0), 1.0, 0.0)
    code_lanes = nn_dot(code_b.astype(BF16), spread_t.astype(BF16))[0:1, :]
    full_lanes = code_lanes * heads + (iota((1, rows), 1) % heads).astype(F32)
    full_col = code_col * heads + (iota((rows, 1), 0) % heads).astype(F32)

    def slot_code(shape, dim):
        i = iota(shape, dim)
        k = i // hb
        o = jnp.where(k % 2 == 1, (k + 1) // 2, n - k // 2)
        t = (z + o) % n
        s = (i // heads) % slots
        return ((t * CAP + 2 * s + c) * heads + i % heads).astype(F32)

    slot_rows = slot_code((n * hb, 1), 0)
    slot_lanes = slot_code((1, n * hb), 1)
    gmat[...] = jnp.where(full_col == slot_lanes, 1.0, 0.0).astype(BF16)

    loads[0].wait()
    pack = jnp.where(slot_rows == full_lanes, 1.0, 0.0).astype(BF16)
    packed = nn_dot(pack, qv[...]).astype(BF16)
    qs[...] = packed.reshape(n, hb, hd)
    qr[0] = packed[0:hb]

    loads[1].wait()
    loads[2].wait()
    pl.semaphore_wait(barrier, n)

    q_copies = []
    for k in range(1, n):
        back = at(-order[k])
        copy = pltpu.make_async_remote_copy(
            src_ref=qs.at[k],
            dst_ref=qr.at[back],
            send_sem=q_send.at[k],
            recv_sem=q_recv.at[back],
            device_id=kv_dev(order[k]),
            device_id_type=MESH,
        )
        q_copies.append((k, back, copy))
    q_by_recv = {back: copy for k, back, copy in q_copies}

    def ring_copy(which, direction, j):
        buf = (kall, vall)[which]
        sign = 1 if direction == 0 else -1
        return pltpu.make_async_remote_copy(
            src_ref=buf.at[at(-sign * j)],
            dst_ref=buf.at[at(-sign * (j + 1))],
            send_sem=ring_send.at[which, direction, j],
            recv_sem=ring_recv.at[which, direction, j],
            device_id=kv_dev(sign),
            device_id_type=MESH,
        )

    ring = {}

    def ring_start(j):
        for which in range(2):
            for direction in range(2):
                if j == half - 1 and which != direction:
                    continue
                copy = ring_copy(which, direction, j)
                copy.start()
                ring[which, direction, j] = copy

    def ring_arrive(j):
        for which in range(2):
            for direction in range(2):
                if (which, direction, j) in ring:
                    ring[which, direction, j].wait_recv()

    ring_start(0)
    for _, _, copy in q_copies:
        copy.start()

    t_copies = []
    for i, (src, dst) in enumerate(((tk_hbm, tk), (tv_hbm, tv))):
        copy = pltpu.make_async_remote_copy(
            src_ref=src,
            dst_ref=dst.at[1],
            send_sem=t_send.at[i],
            recv_sem=t_recv.at[i],
            device_id=partner,
            device_id_type=MESH,
        )
        copy.start()
        t_copies.append(copy)

    def sys_step(first, count, start):
        keys = kall[first : first + count].reshape(count * kall.shape[1], hd)
        vals = vall[first : first + count].reshape(count * kall.shape[1], hd)
        s = nt_dot(qv[...], keys) * unit
        top = jnp.max(s, axis=1, keepdims=True)
        if start:
            m = top
        else:
            old = sys_m[...][:, 0:1]
            m = jnp.maximum(old, top)
        p = jnp.exp2(s - m)
        part = jnp.sum(p, axis=1, keepdims=True)
        num = nn_dot(p.astype(BF16), vals)
        if start:
            sys_l[...] = jnp.broadcast_to(part, (rows, hd))
            sys_acc[...] = num
        else:
            keep = jnp.exp2(old - m)
            sys_l[...] = sys_l[...] * keep + part
            sys_acc[...] = sys_acc[...] * keep + num
        sys_m[...] = jnp.broadcast_to(m, (rows, hd))

    two = 2 * heads

    def suffix_pair(i):
        upper = iota((two, 1), 0) < heads
        base = pl.multiple_of(c * own + i * two, two)
        q2 = qv[pl.ds(base, two), :]
        s = jnp.where(upper, nt_dot(q2, uk[2 * i]), nt_dot(q2, uk[2 * i + 1])) * unit
        limit = jnp.where(upper, len_ref[2 * i], len_ref[2 * i + 1])
        usable = iota((two, suf), 1) < limit
        s = jnp.where(usable, s, NEGATIVE)
        m = jnp.max(s, axis=1, keepdims=True)
        p = jnp.where(usable, jnp.exp2(s - m), 0.0)
        total = jnp.sum(p, axis=1, keepdims=True)
        pb = p.astype(BF16)
        num = jnp.where(upper, nn_dot(pb, uv[2 * i]), nn_dot(pb, uv[2 * i + 1]))
        suf_o[i * two : (i + 1) * two, :] = num / total
        suf_l[i * two : (i + 1) * two, :] = jnp.broadcast_to(m + jnp.log2(total), (two, hd))

    chunk = 512
    r_copies = []

    def task_group(first, count):
        height = count * hb
        for k in range(first, first + count):
            if k > 0:
                q_by_recv[k].wait_recv()
        query = qr[first : first + count].reshape(height, hd)
        top = None
        for b in range(2):
            for i in range(task_half // chunk):
                s = nt_dot(query, tk[b, i * chunk : (i + 1) * chunk, :]) * unit
                base = b * task_half + i * chunk
                scores[0:height, base : base + chunk] = s
                high = jnp.max(s, axis=1, keepdims=True)
                top = high if top is None else jnp.maximum(top, high)
        total = jnp.zeros((height, 1), F32)
        num = jnp.zeros((height, hd), F32)
        for b in range(2):
            for i in range(task_half // chunk):
                base = b * task_half + i * chunk
                p = jnp.exp2(scores[0:height, base : base + chunk] - top)
                total = total + jnp.sum(p, axis=1, keepdims=True)
                num = num + nn_dot(p.astype(BF16), tv[b, i * chunk : (i + 1) * chunk, :])
        result = (num / total).astype(BF16)
        level = jnp.broadcast_to(top + jnp.log2(total), (height, hd))
        for g in range(count):
            k = first + g
            back = at(-order[k])
            block = result[g * hb : (g + 1) * hb]
            lane = iota((hb, hd), 1) == iota((hb, hd), 0) + hb * (back % per)
            line = jnp.sum(
                jnp.where(lane, level[g * hb : (g + 1) * hb], 0.0), axis=0, keepdims=True
            )
            if k == 0:
                rr[0] = block
                sr[0] = line
                continue
            rs[k] = block
            ss[k] = line
            for src, dst, send, recv in ((rs, rr, r_send, r_recv), (ss, sr, s_send, s_recv)):
                copy = pltpu.make_async_remote_copy(
                    src_ref=src.at[k],
                    dst_ref=dst.at[back],
                    send_sem=send.at[k],
                    recv_sem=recv.at[back],
                    device_id=kv_dev(order[k]),
                    device_id_type=MESH,
                )
                copy.start()
                r_copies.append(copy)

    sys_step(0, 1, True)
    loads[3].wait()
    loads[4].wait()
    pairs_left = list(range(own_seqs // 2))
    groups = [(g * half, half) for g in range(2)]
    group_steps = {max(1, half // 2 - 1): 0, max(2, half // 2 + 1): 1}
    for j in range(1, half + 1):
        ring_arrive(j - 1)
        if j < half:
            ring_start(j)
        if j < half:
            sys_step(2 * j - 1, 2, False)
        else:
            sys_step(n - 1, 1, False)
        for _ in range(-(-(own_seqs // 2) // half)):
            if pairs_left:
                suffix_pair(pairs_left.pop(0))
        if j in group_steps:
            if group_steps[j] == 0:
                loads[5].wait()
                loads[6].wait()
                for copy in t_copies:
                    copy.wait_recv()
            task_group(*groups[group_steps[j]])

    for copy in r_copies:
        copy.wait_recv()
    g = gmat[...]
    task_o = nn_dot(g, rr[...].reshape(n * hb, hd))
    weighted = jnp.zeros((rows, hd), F32)
    for b in range(n // per):
        line = jnp.sum(sr[b * per : (b + 1) * per].reshape(per, hd), axis=0, keepdims=True)
        weighted = weighted + g[:, b * hd : (b + 1) * hd].astype(F32) * line
    task_l = jnp.sum(weighted, axis=1, keepdims=True)
    code_i = code_col.astype(jnp.int32)
    mine = code_i % 2 == c
    task_l = jnp.where(mine, task_l, NEGATIVE)
    old = sys_m[...]
    m = jnp.maximum(old, task_l)
    keep = jnp.exp2(old - m)
    gain = jnp.exp2(task_l - m)
    sys_acc[...] = sys_acc[...] * keep + task_o * gain
    den = sys_l[...] * keep + gain
    left_lanes = iota((rows, hd), 1) < hd // 2
    sys_m[...] = jnp.where(left_lanes, m, den)

    theirs = pl.ds(pl.multiple_of((1 - c) * own, own), own)
    ours = pl.ds(pl.multiple_of(c * own, own), own)
    xs[0] = sys_acc[theirs, :]
    xs[1] = sys_m[theirs, :]
    cross = []
    for i in range(2):
        copy = pltpu.make_async_remote_copy(
            src_ref=xs.at[i],
            dst_ref=xr.at[i],
            send_sem=x_send.at[i],
            recv_sem=x_recv.at[i],
            device_id=partner,
            device_id_type=MESH,
        )
        copy.start()
        cross.append(copy)
    a_num = sys_acc[ours, :]
    a_stat = sys_m[ours, :]
    u_o = suf_o[...]
    u_l = suf_l[...][:, 0:1]
    for copy in cross:
        copy.wait_recv()
    b_num = xr[0]
    b_stat = xr[1]
    a_m, a_d = a_stat[:, 0:1], a_stat[:, hd - 1 : hd]
    b_m, b_d = b_stat[:, 0:1], b_stat[:, hd - 1 : hd]
    m = jnp.maximum(jnp.maximum(a_m, b_m), u_l)
    fa, fb, fu = jnp.exp2(a_m - m), jnp.exp2(b_m - m), jnp.exp2(u_l - m)
    den = a_d * fa + b_d * fb + fu
    out_ref[...] = ((a_num * fa + b_num * fb + u_o * fu) / den).astype(out_ref.dtype)

    for copy in ring.values():
        copy.wait_send()
    for _, _, copy in q_copies:
        copy.wait_send()
    for copy in t_copies + r_copies + cross:
        copy.wait_send()


def body(
    queries,
    sys_keys,
    sys_values,
    task_keys,
    task_values,
    suffix_keys,
    suffix_values,
    task_ids,
    suffix_len,
):
    n = lax.axis_size("kv")
    pair, heads, hd = queries.shape
    rows = pair * heads
    shard = sys_keys.shape[1]
    task_half = task_keys.shape[2]
    own_seqs, _, suf, _ = suffix_keys.shape
    own = own_seqs * heads
    half = n // 2
    hb = CAP // 2 * heads
    any_space = pl.BlockSpec(memory_space=pl.ANY)
    vmem = pl.BlockSpec(memory_space=pltpu.VMEM)
    dma = pltpu.SemaphoreType.DMA
    out = pl.pallas_call(
        functools.partial(kernel, n, heads),
        out_shape=jax.ShapeDtypeStruct((own, hd), jnp.bfloat16),
        in_specs=[any_space] * 7 + [vmem, pl.BlockSpec(memory_space=pltpu.SMEM)],
        out_specs=vmem,
        scratch_shapes=[
            pltpu.VMEM((rows, hd), BF16),
            pltpu.VMEM((n, shard, hd), BF16),
            pltpu.VMEM((n, shard, hd), BF16),
            pltpu.VMEM((2, task_half, hd), BF16),
            pltpu.VMEM((2, task_half, hd), BF16),
            pltpu.VMEM((own_seqs, suf, hd), BF16),
            pltpu.VMEM((own_seqs, suf, hd), BF16),
            pltpu.VMEM((n, hb, hd), BF16),
            pltpu.VMEM((n, hb, hd), BF16),
            pltpu.VMEM((n, hb, hd), BF16),
            pltpu.VMEM((n, hb, hd), BF16),
            pltpu.VMEM((n, 1, hd), F32),
            pltpu.VMEM((n, 1, hd), F32),
            pltpu.VMEM((rows, n * hb), BF16),
            pltpu.VMEM((half * hb, 2 * task_half), F32),
            pltpu.VMEM((rows, hd), F32),
            pltpu.VMEM((rows, hd), F32),
            pltpu.VMEM((rows, hd), F32),
            pltpu.VMEM((own, hd), F32),
            pltpu.VMEM((own, hd), F32),
            pltpu.VMEM((2, own, hd), F32),
            pltpu.VMEM((2, own, hd), F32),
            dma((7,)),
            dma((2, 2, half)),
            dma((2, 2, half)),
            dma((n,)),
            dma((n,)),
            dma((n,)),
            dma((n,)),
            dma((n,)),
            dma((n,)),
            dma((2,)),
            dma((2,)),
            dma((2,)),
            dma((2,)),
        ],
        compiler_params=pltpu.CompilerParams(
            collective_id=0, has_side_effects=True, vmem_limit_bytes=56 * 1024 * 1024
        ),
        name="cascade",
    )(
        queries.reshape(rows, hd),
        sys_keys.reshape(shard, hd),
        sys_values.reshape(shard, hd),
        task_keys.reshape(task_half, hd),
        task_values.reshape(task_half, hd),
        suffix_keys.reshape(own_seqs, suf, hd),
        suffix_values.reshape(own_seqs, suf, hd),
        task_ids.reshape(1, pair),
        suffix_len,
    )
    return out.reshape(own_seqs, heads, hd)


def solution(mesh):
    in_specs = (
        P(("replica", "kv"), "head", None),
        P(("replica", "head"), ("kv", "sub"), None),
        P(("replica", "head"), ("kv", "sub"), None),
        P(("replica", "kv"), "head", "sub", None),
        P(("replica", "kv"), "head", "sub", None),
        P(("replica", "kv", "sub"), "head", None, None),
        P(("replica", "kv", "sub"), "head", None, None),
        P(("replica", "kv")),
        P(("replica", "kv", "sub")),
    )
    out_specs = P(("replica", "kv", "sub"), "head", None)
    return jax.shard_map(body, mesh=mesh, in_specs=in_specs, out_specs=out_specs, check_vma=False)
```

time: 171 us -> 88 us (0.51)
  Pallas kernels: 0 us -> 86.5 us
  starting transfers between devices: 64.7 us -> 0 us
  waiting for transfers between devices: 42.4 us -> 0 us
  matrix products: 15.6 us -> 0 us
  local copies, waits for them, and re-layouts: 15.1 us -> 1.38 us
  between operations: 13.7 us -> 0.01 us
  blocking collectives: 10.1 us -> 0 us
  other arithmetic: 9.03 us -> 0 us
    pallas_call x0 -> x1, Pallas kernels: none -> 86.5 us  [body(): pl.pallas_call(functools.partial(kernel, n, heads), out_shape=jax.ShapeDt...]
    all_to_all x4 -> x0, starting transfers between devices: 64.6 us -> none  [the longest x1 44.2 us: body(): lax.all_to_all(outgoing, 'kv', split_axis=0, concat_axis=0, tiled=True)]
    all_to_all x4 -> x0, waiting for transfers between devices: 41.6 us -> none  [the longest x1 12.5 us: body(): lax.all_to_all(parted_task[2], 'kv', split_axis=0, concat_axis=0, tiled=T...]
    dot_general x6 -> x0, matrix products: 15.6 us -> none  [the longest x2 7.03 us: shared_partial(): jnp.einsum('rkgl,kld->rkgd', weights.astype(jnp.bfloat16), level_values,...]
    all_to_all x1 -> x0, blocking collectives: 10.1 us -> none  [in_one_piece(): lax.all_to_all(both, axis, split_axis=split_dim, concat_axis=concat_dim,...]
    reduce_sum x6 -> x0, other arithmetic: 5 us -> none  [the longest x2 3.64 us: shared_partial(): totals = jnp.sum(weights, axis=3)]
    reshape x6 -> x0, local copies, waits for them, and re-layouts: 3.11 us -> none  [the longest x5 2.37 us: split_lead(): member.reshape((blocks, member.shape[0] // blocks) + member.shape[1:])]
    scatter x1 -> x0, local copies, waits for them, and re-layouts: 2.54 us -> none  [body(): outgoing = jnp.zeros((owners * CAP, kv_heads, group_size, head_dim), jnp....]
  transfers between devices with their start and end apart: 5 -> 0, of which waited for: 5 -> 0; matrix products, arithmetic and copies ran while one was open for 14% -> 0% of each run, Pallas kernels for 0% -> 0%
where the time goes in v1:
time: 88 us; the launch traced here: 87.8 us
  Pallas kernels  86.5 us (98%)
  local copies, waits for them, and re-layouts  1.38 us (2%)
    pallas_call x1, Pallas kernels, body(): pl.pallas_call(functools.partial(kernel, n, heads), out_shape=jax.ShapeDt...  86.5 us

profile of v1, /device:TPU:65, one launch (start us, length us, event | category | flops | bytes accessed | tf_op | source)
XLA Modules:
  0.0 87.8 jit_solution(4340870284251892387)
XLA Ops:
  0.0 86.5 %cascade.1 = bf16[128,128]{1,0:T(8,128)(2,1)} custom-call(bf16[256,128]{1,0:T(8,128)(2,1)} %bitcast.14, bf16[128,128]{1,0:T(8,128)(2,1)} %bitcast.15, bf16[128,128]{1,0:T(8,128)(2,1)} %bitcast.16, bf16[2048,128]{1,0:T(8,128)(2,1)} %bitcast.11, bf16[2048,128]{1,0:T(8,128)(2,1)} %bitcast.12, bf16[16,512,128]{2,1,0:T(8,128)(2,1)} %bitcast.9, ...), custom_call_target="tpu_custom_call" | custom-call | tf_op jit(solution)/shard_map/cascade/pallas_call | solution.py:429
  86.5 1.4 %copy.11 = bf16[16,8,128]{2,1,0:T(8,128)(2,1)} copy(bf16[16,8,128]{2,1,0:T(8,128)(2,1)} %bitcast.13) | data formatting | bytes 65536

commit v2 on v1

v2 whole, which is shorter than its diff:
```python
import functools
import math

import jax
import jax.numpy as jnp
from jax import lax
from jax.experimental import pallas as pl
from jax.experimental.pallas import tpu as pltpu
from jax.sharding import PartitionSpec as P

CAP = 8
NEGATIVE = -1e30
RING_ORDERS = [28518, 27199, 22895, 19710, 21998, 26525, 22453, 27891, 29613, 24405, 32398, 30166, 24409, 16242, 30692, 32736]
MESH = pl.DeviceIdType.MESH
F32 = jnp.float32
BF16 = jnp.bfloat16


def nt_dot(a, b):
    return lax.dot_general(a, b, (((1,), (1,)), ((), ())), preferred_element_type=F32)


def nn_dot(a, b):
    return lax.dot_general(a, b, (((1,), (0,)), ((), ())), preferred_element_type=F32)


def iota(shape, dim):
    return lax.broadcasted_iota(jnp.int32, shape, dim)


def kernel(
    n,
    heads,
    q_hbm,
    sk_hbm,
    sv_hbm,
    tk_hbm,
    tv_hbm,
    uk_hbm,
    uv_hbm,
    ids_hbm,
    len_hbm,
    out_ref,
    qv,
    kall,
    vall,
    tk,
    tv,
    uk,
    uv,
    ids_ref,
    len_ref,
    qs,
    qr,
    rs,
    rr,
    ss,
    sr,
    gmat,
    scores,
    part_m,
    part_l,
    part_num,
    suf_l,
    suf_o,
    xs,
    xr,
    outv,
    local_sem,
    ring_send,
    ring_recv,
    q_send,
    q_recv,
    r_send,
    r_recv,
    s_send,
    s_recv,
    t_send,
    t_recv,
    x_send,
    x_recv,
    k_send,
    k_recv,
    mate_sem,
    in_sem,
    right_sem,
    left_sem,
):
    z = lax.axis_index("kv")
    c = lax.axis_index("sub")
    half = n // 2
    rows, hd = q_hbm.shape
    pair = rows // heads
    own = rows // 2
    own_seqs, suf, _ = uk_hbm.shape
    task_half = tk_hbm.shape[0]
    hb = CAP * heads
    per = hd // hb
    unit = math.log2(math.e) / math.sqrt(hd)

    order = [0]
    for d in range(1, half):
        order += [d, n - d]
    order.append(half)
    place = {o: k for k, o in enumerate(order)}

    def at(offset):
        return place[offset % n]

    def kv_dev(offset):
        return {"kv": lax.rem(z + (offset % n), n)}

    partner = {"sub": 1 - c}

    def remote(src, dst, send, recv, device):
        return pltpu.make_async_remote_copy(
            src_ref=src,
            dst_ref=dst,
            send_sem=send,
            recv_sem=recv,
            device_id=device,
            device_id_type=MESH,
        )

    def load(i, src, dst):
        return pltpu.make_async_copy(src, dst, local_sem.at[i])

    load_q = load(0, q_hbm, qv)
    load_len = load(1, len_hbm, len_ref)
    load_uk = load(2, uk_hbm, uk)
    load_uv = load(3, uv_hbm, uv)
    load_k = load(4, sk_hbm, kall.at[0, 1])
    load_v = load(5, sv_hbm, vall.at[0, 1])
    load_ids = load(4, ids_hbm, ids_ref)
    load_tk = load(5, tk_hbm, tk.at[0])
    load_tv = load(6, tv_hbm, tv.at[0])
    load_k0 = load(7, sk_hbm, kall.at[0, 0])
    load_v0 = load(8, sv_hbm, vall.at[0, 0])

    t_copies = [
        remote(src, dst.at[1], t_send.at[i], t_recv.at[i], partner)
        for i, (src, dst) in enumerate(((tk_hbm, tk), (tv_hbm, tv)))
    ]
    k_copies = [
        remote(buf.at[0, 0], buf.at[0, 0], k_send.at[i], k_recv.at[i], partner)
        for i, buf in enumerate((kall, vall))
    ]
    barrier = pltpu.get_barrier_semaphore()

    two = 2 * heads

    def suffix_pair(i):
        upper = iota((two, 1), 0) < heads
        base = pl.multiple_of(c * own + i * two, two)
        q2 = qv[pl.ds(base, two), :]
        s = jnp.where(upper, nt_dot(q2, uk[2 * i]), nt_dot(q2, uk[2 * i + 1])) * unit
        limit = jnp.where(upper, len_ref[2 * i], len_ref[2 * i + 1])
        usable = iota((two, suf), 1) < limit
        s = jnp.where(usable, s, NEGATIVE)
        m = jnp.max(s, axis=1, keepdims=True)
        p = jnp.where(usable, jnp.exp2(s - m), 0.0)
        total = jnp.sum(p, axis=1, keepdims=True)
        pb = p.astype(BF16)
        num = jnp.where(upper, nn_dot(pb, uv[2 * i]), nn_dot(pb, uv[2 * i + 1]))
        spot = pl.ds(pl.multiple_of(i * two, two), two)
        suf_o[spot, :] = num / total
        suf_l[spot, :] = jnp.broadcast_to(m + jnp.log2(total), (two, hd))

    def suffix_loads():
        load_len.wait()
        load_uk.wait()
        load_uv.wait()

    def suffixes():
        suffix_loads()

        @pl.loop(0, own_seqs // 2)
        def _(i):
            suffix_pair(i)

    left_lanes = iota((rows, hd), 1) < hd // 2

    reach = (n // 3, n - 1 - n // 3)

    def ring_copy(which, core, direction, j):
        buf = (kall, vall)[which]
        sign = 1 if direction == 0 else -1
        return remote(
            buf.at[(-sign * j) % n, core],
            buf.at[(-sign * (j + 1)) % n, core],
            ring_send.at[which],
            ring_recv.at[which, core, (-sign * (j + 1)) % n],
            kv_dev(sign),
        )

    ring = {
        (which, core, direction, j): ring_copy(which, core, direction, j)
        for which in range(2)
        for core in range(2)
        for direction in range(2)
        for j in range(1)
    }

    def ring_first(core, direction):
        for which in range(2):
            ring[which, core, direction, 0].start()

    def ring_open():
        load_k.wait()
        load_v.wait()
        for core in (1, 0):
            if core == 0:
                for copy in k_copies:
                    copy.wait_recv()

            @pl.when(z > 0)
            def _():
                ring_first(core, 1)

            @pl.when(z == n - 1)
            def _():
                ring_first(core, 0)

        pl.when(z > 0)(load_q.wait)
        sys_step(kall[0], vall[0], True)
        @pl.when(z < n - 1)
        def _():
            pl.semaphore_wait(right_sem, 1)
            for core in (1, 0):
                ring_first(core, 0)

        @pl.when(z == 0)
        def _():
            pl.semaphore_wait(left_sem, 1)
            for core in (1, 0):
                ring_first(core, 1)

        pl.when(z > 0)(suffix_loads)

    def ring_orders():
        if n == len(RING_ORDERS):
            return RING_ORDERS
        gap, hop, wire = 2.7, 2.1, 1.4
        come = [gap * (n - 1) + 1.0] + [gap * i for i in range(1, n)]
        when = {(d, 0, i): come[i] for d in range(2) for i in range(n)}
        for j in range(1, n):
            for d in range(2):
                for i in range(n):
                    source = (i - 1) % n if d == 0 else (i + 1) % n
                    at_source = max(when[d, j - 1, source], come[source], come[i] if i else 0) + hop
                    when[d, j, i] = max(at_source, when[d, j - 1, i] + wire)
        masks = []
        for i in range(n):
            events = sorted((when[d, j, i], j, d) for d in range(2) for j in range(1, reach[d] + 1))
            masks.append(sum(d << k for k, (_, _, d) in enumerate(events)))
        return masks

    def slot(d, j):
        return d * j + (1 - d) * ((n - j) % n)

    def ring_moves(d, j):
        def piece(which, core, step):
            buf = (kall, vall)[which]
            return remote(
                buf.at[slot(d, step), core],
                buf.at[slot(d, step + 1), core],
                ring_send.at[which],
                ring_recv.at[which, core, slot(d, step + 1)],
                {"kv": lax.rem(z + 1 - 2 * d + n, n)},
            )

        for core in (1, 0):
            for which in range(2):
                piece(which, core, j - 1).wait_recv()

                @pl.when(j < d * reach[1] + (1 - d) * reach[0])
                def _():
                    piece(which, core, j).start()

    def sys_step(keys, vals, start):
        keys = keys.reshape(-1, hd)
        vals = vals.reshape(-1, hd)
        s = nt_dot(qv[...], keys) * unit
        top = jnp.max(s, axis=1, keepdims=True)
        if start:
            m = top
        else:
            old = part_m[...][:, 0:1]
            m = jnp.maximum(old, top)
        p = jnp.exp2(s - m)
        part = jnp.sum(p, axis=1, keepdims=True)
        num = nn_dot(p.astype(BF16), vals)
        if start:
            part_l[...] = jnp.broadcast_to(part, (rows, hd))
            part_num[...] = num
        else:
            keep = jnp.exp2(old - m)
            part_l[...] = part_l[...] * keep + part
            part_num[...] = part_num[...] * keep + num
        part_m[...] = jnp.broadcast_to(m, (rows, hd))

    @pl.when(c == 1)
    def _():
        @pl.when(z < n - 1)
        def _():
            pl.semaphore_signal(barrier, inc=1, device_id=kv_dev(1), device_id_type=MESH)

        @pl.when(z == 0)
        def _():
            pl.semaphore_signal(barrier, inc=1, device_id=kv_dev(-1), device_id_type=MESH)

        for copy in (load_k, load_v, load_q, load_len, load_uk, load_uv):
            copy.start()
        @pl.when(z == 0)
        def _():
            load_q.wait()
            suffixes()

        pl.semaphore_wait(barrier, 1 + (z + n - 1) // n + (z + 1) // n)
        pl.semaphore_signal(mate_sem, inc=1, device_id=partner, device_id_type=MESH)

        @pl.when(z > 0)
        def _():
            pl.semaphore_signal(right_sem, inc=1, device_id=kv_dev(-1), device_id_type=MESH)

        @pl.when(z == n - 1)
        def _():
            pl.semaphore_signal(left_sem, inc=1, device_id=kv_dev(1), device_id_type=MESH)

        for copy in t_copies:
            copy.start()
        ring_open()
        first_in = half
        mask = 0
        for i, value in enumerate(ring_orders()):
            mask = mask + jnp.where(z == i, value, 0)

        @pl.loop(0, half, init_carry=(jnp.int32(0), mask))
        def _(i, carry):
            lefts, bits = carry
            at_once = z < first_in
            paired = i < half - 1

            def event(e, lefts, bits):
                d = bits % 2
                j = d * (lefts + 1) + (1 - d) * (2 * i + e - lefts + 1)
                ring_moves(d, j)
                return slot(d, j), lefts + d, bits // 2

            first, lefts, bits = event(0, lefts, bits)

            @pl.when(paired)
            def _():
                second, _, _ = event(1, lefts, bits)

                @pl.when(at_once)
                def _():
                    sys_step(
                        jnp.concatenate([kall[first], kall[second]], axis=0),
                        jnp.concatenate([vall[first], vall[second]], axis=0),
                        False,
                    )

            @pl.when(jnp.logical_and(at_once, jnp.logical_not(paired)))
            def _():
                sys_step(kall[first], vall[first], False)

            lefts, bits = lefts + bits % 2, bits // 2

            @pl.when(jnp.logical_and(jnp.logical_and(z > 0, at_once), i < own_seqs // 2))
            def _():
                suffix_pair(i)

            return lefts, bits

        @pl.when(z >= first_in)
        def _():
            @pl.loop(1, half)
            def _(i):
                spot = pl.ds(2 * i - 1, 2)
                sys_step(kall[spot], vall[spot], False)

            @pl.loop(0, min(half, own_seqs // 2))
            def _(i):
                suffix_pair(i)

            sys_step(kall[n - 1], vall[n - 1], False)

        @pl.when(z > 0)
        def _():
            @pl.loop(half, max(own_seqs // 2, half))
            def _(i):
                suffix_pair(i)

        part_m[...] = jnp.where(left_lanes, part_m[...], part_l[...])

    v = z - 1 + (1 - (z + n - 1) // n) * (n - 1) + z // (n - 1)

    def nth(i):
        if i == 0:
            return v
        below = (v - i + n) // n
        lower = v - (i + 1) // 2 if i % 2 == 1 else i // 2 - 1
        return below * lower + (1 - below) * i

    def kv_of(k):
        return (k + 1) * (1 - k // (n - 2)) + (k // (n - 1)) * (n - 1)

    def dev(k):
        return {"kv": kv_of(k)}

    def q_copy(k):
        return remote(qs.at[k], qr.at[v], q_send.at[0], q_recv.at[v], dev(k))

    def q_arrival(k):
        return remote(qs.at[k], qr.at[k], q_send.at[0], q_recv.at[k], dev(k))

    def r_copy(k):
        return [
            remote(rs.at[k], rr.at[v], r_send.at[0], r_recv.at[0], dev(k)),
            remote(ss.at[k], sr.at[v], s_send.at[0], s_recv.at[0], dev(k)),
        ]

    others = pl.ds(0, n - 1)
    mate_dev = {"sub": 1 - c}
    q_all = remote(qs.at[others], qr.at[others], q_send.at[0], q_recv.at[0], mate_dev)
    r_all = [
        remote(rs.at[others], rr.at[others], r_send.at[0], r_recv.at[0], mate_dev),
        remote(ss.at[others], sr.at[others], s_send.at[0], s_recv.at[0], mate_dev),
    ]
    ring_all = [
        remote(
            buf.at[others], buf.at[others], ring_send.at[i], ring_recv.at[i, 0, 0], mate_dev
        )
        for i, buf in enumerate((kall, vall))
    ]

    chunk = 512

    def task_group(first, count):
        height = count * hb
        names = [nth(i) for i in range(first, first + count)]
        for i in range(count):
            if first + i > 0:
                q_arrival(names[i]).wait_recv()
        query = jnp.concatenate([qr[k] for k in names], axis=0)
        top = None
        for b in range(2):
            for i in range(task_half // chunk):
                s = nt_dot(query, tk[b, i * chunk : (i + 1) * chunk, :]) * unit
                base = b * task_half + i * chunk
                scores[0:height, base : base + chunk] = s
                high = jnp.max(s, axis=1, keepdims=True)
                top = high if top is None else jnp.maximum(top, high)
        total = jnp.zeros((height, 1), F32)
        num = jnp.zeros((height, hd), F32)
        for b in range(2):
            for i in range(task_half // chunk):
                base = b * task_half + i * chunk
                p = jnp.exp2(scores[0:height, base : base + chunk] - top)
                total = total + jnp.sum(p, axis=1, keepdims=True)
                num = num + nn_dot(p.astype(BF16), tv[b, i * chunk : (i + 1) * chunk, :])
        result = (num / total).astype(BF16)
        level = jnp.broadcast_to(top + jnp.log2(total), (height, hd))
        for g in range(count):
            k = names[g]
            block = result[g * hb : (g + 1) * hb]
            lane = iota((hb, hd), 1) == iota((hb, hd), 0) + hb * (v % per)
            line = jnp.sum(
                jnp.where(lane, level[g * hb : (g + 1) * hb], 0.0), axis=0, keepdims=True
            )
            if first + g == 0:
                rr[v] = block
                sr[v] = line
                continue
            rs[k] = block
            ss[k] = line
            for copy in r_copy(k):
                copy.start()

    near = 5

    def ask_above(first, last, rest):
        for k in range(first, last):
            chosen = k > v + near if rest else jnp.logical_and(k > v, k <= v + near)

            @pl.when(chosen)
            def _():
                pl.semaphore_wait(in_sem.at[k], 1)
                q_copy(k).start()

    def enter():
        @pl.when(v > 0)
        def _():
            pl.semaphore_wait(barrier, 1 + v // (n - 1))

        @pl.when(v < n - 2)
        def _():
            pl.semaphore_signal(barrier, inc=1, device_id=dev(v + 1), device_id_type=MESH)

        @pl.when(v == n - 3)
        def _():
            pl.semaphore_signal(barrier, inc=1, device_id=dev(n - 1), device_id_type=MESH)

        for i in range(1, n):

            @pl.when(i <= v)
            def _():
                pl.semaphore_signal(
                    in_sem.at[v], inc=1, device_id=dev(nth(i)), device_id_type=MESH
                )

    @pl.when(c == 0)
    def _():
        mate = {"sub": 1}
        pl.semaphore_signal(barrier, inc=1, device_id=mate, device_id_type=MESH)

        @pl.when(z == 0)
        def _():
            pl.semaphore_signal(barrier, inc=1, device_id=dev(n - 1), device_id_type=MESH)

        for copy in (load_ids, load_q, load_k0, load_v0, load_len, load_uk, load_uv, load_tk, load_tv):
            copy.start()

        def give_keys():
            pl.semaphore_wait(mate_sem, 1)
            load_k0.wait()
            load_v0.wait()
            for copy in k_copies:
                copy.start()

        pl.when(z == 0)(give_keys)
        enter()
        pl.when(z == n - 1)(give_keys)

        load_ids.wait()
        ids_row = ids_ref[...].astype(F32)
        ids_b = jnp.broadcast_to(ids_row, (pair, pair))
        eye = iota((pair, pair), 0) == iota((pair, pair), 1)
        ids_col = jnp.sum(jnp.where(eye, ids_b, 0.0), axis=1, keepdims=True)
        before = iota((pair, pair), 0) < iota((pair, pair), 1)
        same = jnp.logical_and(ids_col == ids_b, before)
        rank_row = jnp.sum(jnp.where(same, 1.0, 0.0), axis=0, keepdims=True)
        code_row = ids_row * CAP + rank_row
        code_b = jnp.broadcast_to(code_row, (pair, pair))
        spread = iota((rows, pair), 0) // heads == iota((rows, pair), 1)
        code_col = jnp.sum(
            jnp.where(spread, jnp.broadcast_to(code_row, (rows, pair)), 0.0), axis=1, keepdims=True
        )
        spread_t = jnp.where(iota((pair, rows), 1) // heads == iota((pair, rows), 0), 1.0, 0.0)
        code_lanes = nn_dot(code_b.astype(BF16), spread_t.astype(BF16))[0:1, :]
        full_lanes = code_lanes * heads + (iota((1, rows), 1) % heads).astype(F32)
        full_col = code_col * heads + (iota((rows, 1), 0) % heads).astype(F32)

        def slot_code(shape, dim):
            i = iota(shape, dim)
            return (kv_of(i // hb) * hb + i % hb).astype(F32)

        load_q.wait()
        pack = jnp.where(slot_code((n * hb, 1), 0) == full_lanes, 1.0, 0.0).astype(BF16)
        packed = nn_dot(pack, qv[...]).astype(BF16)
        qs[...] = packed.reshape(n, hb, hd)
        for i in reversed(range(1, n)):

            @pl.when(i <= v)
            def _():
                q_copy(nth(i)).start()

        pl.when(v < n - 2)(give_keys)
        qr[v] = qs[v]
        gmat[...] = jnp.where(full_col == slot_code((1, n * hb), 1), 1.0, 0.0).astype(BF16)
        pl.when(v < n - 2)(suffixes)
        ask_above(1, n, False)
        load_tk.wait()
        load_tv.wait()
        for copy in t_copies:
            copy.wait_recv()
        done, asked = 0, 1
        while done < n:
            count = half // 2 if done < half else max(half // 4, 1)
            ahead = min(done + count + 4, n)
            ask_above(asked, ahead, True)
            asked = ahead
            if done == 0:
                pl.when(v >= n - 2)(suffixes)
            task_group(done, count)
            done += count

        for copy in r_all:
            copy.wait_recv()

        g = gmat[...]
        part_num[...] = nn_dot(g, rr[...].reshape(n * hb, hd))
        weighted = jnp.zeros((rows, hd), F32)
        for b in range(n // per):
            line = jnp.sum(sr[b * per : (b + 1) * per].reshape(per, hd), axis=0, keepdims=True)
            weighted = weighted + g[:, b * hd : (b + 1) * hd].astype(F32) * line
        task_l = jnp.sum(weighted, axis=1, keepdims=True)
        part_m[...] = jnp.where(left_lanes, task_l, 1.0)

    theirs = pl.ds(pl.multiple_of((1 - c) * own, own), own)
    ours = pl.ds(pl.multiple_of(c * own, own), own)
    xs[0] = part_num[theirs, :]
    xs[1] = part_m[theirs, :]
    cross = [remote(xs.at[i], xr.at[i], x_send.at[i], x_recv.at[i], partner) for i in range(2)]
    for copy in cross:
        copy.start()
    a_num = part_num[ours, :]
    a_stat = part_m[ours, :]
    u_o = suf_o[...]
    u_l = suf_l[...][:, 0:1]
    for copy in cross:
        copy.wait_recv()
    b_num = xr[0]
    b_stat = xr[1]
    a_m, a_d = a_stat[:, 0:1], a_stat[:, hd - 1 : hd]
    b_m, b_d = b_stat[:, 0:1], b_stat[:, hd - 1 : hd]
    m = jnp.maximum(jnp.maximum(a_m, b_m), u_l)
    fa, fb, fu = jnp.exp2(a_m - m), jnp.exp2(b_m - m), jnp.exp2(u_l - m)
    den = a_d * fa + b_d * fb + fu
    outv[...] = ((a_num * fa + b_num * fb + u_o * fu) / den).astype(BF16)
    give = pltpu.make_async_copy(outv, out_ref, local_sem.at[0])
    give.start()

    for copy in cross:
        copy.wait_send()
    give.wait()

    @pl.when(c == 1)
    def _():
        for copy in ring_all + t_copies:
            copy.wait_send()

    @pl.when(c == 0)
    def _():
        for copy in k_copies + [q_all] + r_all:
            copy.wait_send()


def body(
    queries,
    sys_keys,
    sys_values,
    task_keys,
    task_values,
    suffix_keys,
    suffix_values,
    task_ids,
    suffix_len,
):
    n = lax.axis_size("kv")
    pair, heads, hd = queries.shape
    rows = pair * heads
    shard = sys_keys.shape[1]
    task_half = task_keys.shape[2]
    own_seqs, _, suf, _ = suffix_keys.shape
    own = own_seqs * heads
    half = n // 2
    hb = CAP * heads
    any_space = pl.BlockSpec(memory_space=pl.ANY)
    dma = pltpu.SemaphoreType.DMA
    out = pl.pallas_call(
        functools.partial(kernel, n, heads),
        out_shape=jax.ShapeDtypeStruct((own, hd), jnp.bfloat16),
        in_specs=[any_space] * 9,
        out_specs=any_space,
        scratch_shapes=[
            pltpu.VMEM((rows, hd), BF16),
            pltpu.VMEM((n, 2, shard, hd), BF16),
            pltpu.VMEM((n, 2, shard, hd), BF16),
            pltpu.VMEM((2, task_half, hd), BF16),
            pltpu.VMEM((2, task_half, hd), BF16),
            pltpu.VMEM((own_seqs, suf, hd), BF16),
            pltpu.VMEM((own_seqs, suf, hd), BF16),
            pltpu.VMEM((1, pair), jnp.int32),
            pltpu.SMEM((own_seqs,), jnp.int32),
            pltpu.VMEM((n, hb, hd), BF16),
            pltpu.VMEM((n, hb, hd), BF16),
            pltpu.VMEM((n, hb, hd), BF16),
            pltpu.VMEM((n, hb, hd), BF16),
            pltpu.VMEM((n, 1, hd), F32),
            pltpu.VMEM((n, 1, hd), F32),
            pltpu.VMEM((rows, n * hb), BF16),
            pltpu.VMEM((half // 2 * hb, 2 * task_half), F32),
            pltpu.VMEM((rows, hd), F32),
            pltpu.VMEM((rows, hd), F32),
            pltpu.VMEM((rows, hd), F32),
            pltpu.VMEM((own, hd), F32),
            pltpu.VMEM((own, hd), F32),
            pltpu.VMEM((2, own, hd), F32),
            pltpu.VMEM((2, own, hd), F32),
            pltpu.VMEM((own, hd), BF16),
            dma((9,)),
            dma((2,)),
            dma((2, 2, n)),
            dma((1,)),
            dma((n,)),
            dma((1,)),
            dma((1,)),
            dma((1,)),
            dma((1,)),
            dma((2,)),
            dma((2,)),
            dma((2,)),
            dma((2,)),
            dma((2,)),
            dma((2,)),
            pltpu.SemaphoreType.REGULAR,
            pltpu.SemaphoreType.REGULAR((n,)),
            pltpu.SemaphoreType.REGULAR,
            pltpu.SemaphoreType.REGULAR,
        ],
        compiler_params=pltpu.CompilerParams(
            collective_id=0, has_side_effects=True, vmem_limit_bytes=56 * 1024 * 1024
        ),
        name="cascade",
    )(
        queries.reshape(rows, hd),
        sys_keys.reshape(shard, hd),
        sys_values.reshape(shard, hd),
        task_keys.reshape(task_half, hd),
        task_values.reshape(task_half, hd),
        suffix_keys.reshape(own_seqs, suf, hd),
        suffix_values.reshape(own_seqs, suf, hd),
        task_ids.reshape(1, pair),
        suffix_len,
    )
    return out.reshape(own_seqs, heads, hd)


def solution(mesh):
    in_specs = (
        P(("replica", "kv"), "head", None),
        P(("replica", "head"), ("kv", "sub"), None),
        P(("replica", "head"), ("kv", "sub"), None),
        P(("replica", "kv"), "head", "sub", None),
        P(("replica", "kv"), "head", "sub", None),
        P(("replica", "kv", "sub"), "head", None, None),
        P(("replica", "kv", "sub"), "head", None, None),
        P(("replica", "kv")),
        P(("replica", "kv", "sub")),
    )
    out_specs = P(("replica", "kv", "sub"), "head", None)
    return jax.shard_map(body, mesh=mesh, in_specs=in_specs, out_specs=out_specs, check_vma=False)
```

time: 88 us -> 70.9 us (0.81)
  Pallas kernels: 86.5 us -> 69.4 us
    pallas_call x1, Pallas kernels: 86.5 us -> 69.4 us  [body(): pl.pallas_call(functools.partial(kernel, n, heads), out_shape=jax.ShapeDt...]
where the time goes in v2:
time: 70.9 us; the launch traced here: 70.8 us
  Pallas kernels  69.4 us (98%)
  local copies, waits for them, and re-layouts  1.38 us (2%)
    pallas_call x1, Pallas kernels, body(): pl.pallas_call(functools.partial(kernel, n, heads), out_shape=jax.ShapeDt...  69.4 us

profile of v2, /device:TPU:65, one launch (start us, length us, event | category | flops | bytes accessed | tf_op | source)
XLA Modules:
  0.0 70.8 jit_solution(12718772894982863621)
XLA Ops:
  0.0 69.4 %cascade.1 = bf16[128,128]{1,0:T(8,128)(2,1)} custom-call(bf16[256,128]{1,0:T(8,128)(2,1)} %bitcast.14, bf16[128,128]{1,0:T(8,128)(2,1)} %bitcast.15, bf16[128,128]{1,0:T(8,128)(2,1)} %bitcast.16, bf16[2048,128]{1,0:T(8,128)(2,1)} %bitcast.11, bf16[2048,128]{1,0:T(8,128)(2,1)} %bitcast.12, bf16[16,512,128]{2,1,0:T(8,128)(2,1)} %bitcast.9, ...), custom_call_target="tpu_custom_call" | custom-call | tf_op jit(solution)/shard_map/cascade/pallas_call | solution.py:662
  69.4 1.4 %copy.11 = bf16[16,8,128]{2,1,0:T(8,128)(2,1)} copy(bf16[16,8,128]{2,1,0:T(8,128)(2,1)} %bitcast.13) | data formatting | bytes 65536
